TPU v7x, 32 devices: a whole 2x2x4 slice. The times are simulated.
32 devices in a mesh: groups: 2 (over x), seq: 16 (over z, y, core).
Axes of the slice: x: 2, y: 2, z: 4, core: 2. Of those that a mesh axis runs over, the one named last changes fastest.
Arguments:
- mixed_input: bfloat16 [8192, 2816], P(('groups', 'seq')), parts along dimension 0, may hold values from -6 to 6
- step_raw: float32 [40, 8192], P(None, ('groups', 'seq')), parts along dimension 1, may hold values from -2.5 to 5.5
- conv_weight: float32 [4, 2816], replicated, may hold values from -1.5 to 1.5
- conv_bias: float32 [2816], replicated, may hold values from -1.2 to 1.2
- step_bias: float32 [40], replicated, may hold values from -5 to -3
- decay_log: float32 [40], replicated, may hold values from -12 to 1
- skip_gain: float32 [40], replicated, may hold values from 0.5 to 1.5
- result_cotangent: bfloat16 [8192, 2560], P(('groups', 'seq')), parts along dimension 0, may hold values from -1.1953125 to 1.1953125
- entry_state: float32 [32, 40, 64, 128], P(('groups', 'seq')), parts along dimension 0, may hold values from -3 to 3
Outputs:
- input_grad: float32 [8192, 2816], P(('groups', 'seq')), parts along dimension 0
- step_grad: float32 [40, 8192], P(None, ('groups', 'seq')), parts along dimension 1
- kernel_grad: float32 [8, 2816], P('groups'), parts along dimension 0
- offset_grad: float32 [5632], P('groups'), parts along dimension 0
- bias_grad: float32 [80], P('groups'), parts along dimension 0
- decay_grad: float32 [80], P('groups'), parts along dimension 0
- skip_grad: float32 [80], P('groups'), parts along dimension 0
There are 2 independent parts, one for each index of `groups`. A program takes and returns all parts, laid end to end along the dimension named above; an argument that names none is the same for every part. Nothing has to cross between parts.
All inputs are finite; a program needn't handle non-finite values.
Results may differ from a plain program's by a relative error of at most 0.0003.
Values may be sent and summed in bfloat16 or wider, within the bound.
A program may use at most 384 MiB of HBM per device.

v0:
```python
import functools

import jax
import jax.numpy as jnp
from jax import lax
from jax.experimental import pallas as pl
from jax.experimental.pallas import tpu as pltpu
from jax.sharding import PartitionSpec as P

F32 = jnp.float32
BF16 = jnp.bfloat16
LANES = 128
WIDE = 256
LOG2E = 1.4426950408889634
MESH = pl.DeviceIdType.MESH


def split2(v):
    hi = v.astype(BF16)
    return hi, (v - hi.astype(F32)).astype(BF16)


def split3(v):
    hi = v.astype(BF16)
    rest = v - hi.astype(F32)
    mid = rest.astype(BF16)
    return hi, mid, (rest - mid.astype(F32)).astype(BF16)


def nn(a, b):
    return lax.dot_general(a, b, (((1,), (0,)), ((), ())), preferred_element_type=F32)


def nt(a, b):
    return lax.dot_general(a, b, (((1,), (1,)), ((), ())), preferred_element_type=F32)


def both(dot, a, b):
    return dot(a[0], b[0]) + dot(a[1], b[0]) + dot(a[0], b[1])


def iota(shape, dim):
    return lax.broadcasted_iota(jnp.int32, shape, dim)


def body(
    n, heads, width,
    xin, raw, conv_w, conv_b, cols, skip, cot, state,
    ig, step_g, kg_out, off_out, small_out,
    ext, x_s, ds_s, run_s, steps_s, p128, run_t, dxs_s, st_hi, st_lo, gt, et, f_s,
    gram, dgram, dpos, acc_c, acc_b, q_acc, r_acc, last_acc, skip_acc, dconv, halo_in, bf_buf, bf_in,
    send_sem, recv_sem, halo_sem, back_sem, sum_sem,
):
    tok = xin.shape[0]
    chan = xin.shape[1]
    inner = heads * width
    pairs = inner // LANES
    quads = inner // WIDE
    idx = lax.axis_index("seq")
    rounds = n.bit_length() - 1
    has_prev, has_next = idx > 0, idx < n - 1

    def to(where):
        return {"seq": where}

    barrier = pltpu.get_barrier_semaphore()

    @pl.when(has_prev)
    def _():
        pl.semaphore_signal(barrier, inc=1, device_id=to(idx - 1), device_id_type=MESH)

    @pl.when(has_next)
    def _():
        pl.semaphore_signal(barrier, inc=1, device_id=to(idx + 1), device_id_type=MESH)

    def partner(k):
        bit = 1 << k
        return jnp.where((idx // bit) % 2 == 0, idx + bit, idx - bit)

    for k in range(1, rounds):
        pl.semaphore_signal(barrier, inc=1, device_id=to(partner(k)), device_id_type=MESH)
    pl.semaphore_wait(barrier, rounds - 1 + has_prev.astype(jnp.int32) + has_next.astype(jnp.int32))

    halo_copy = pltpu.make_async_remote_copy(
        src_ref=xin.at[pl.ds(tok - 16, 16)], dst_ref=halo_in,
        send_sem=halo_sem.at[0], recv_sem=halo_sem.at[1],
        device_id=to(idx + 1), device_id_type=MESH,
    )

    @pl.when(has_next)
    def _():
        halo_copy.start()

    z = raw[...] + cols[:, 0:1]
    steps_t = jnp.maximum(z, 0.0) + jnp.log1p(jnp.exp(-jnp.abs(z)))
    rate = jnp.exp(cols[:, 1:2])
    p128[...] = jnp.zeros_like(p128)
    p128[0:heads, :] = -steps_t * rate * LOG2E
    upper = jnp.where(iota((tok, tok), 0) <= iota((tok, tok), 1), 1.0, 0.0).astype(BF16)
    lower = jnp.where(iota((tok, tok), 0) >= iota((tok, tok), 1), 1.0, 0.0).astype(BF16)
    parts = split3(p128[...])
    run_rows = nn(parts[0], upper) + nn(parts[1], upper) + nn(parts[2], upper)
    run_t[...] = run_rows
    run_col = split3(run_rows.T)
    p128[0:heads, :] = steps_t
    steps_col = p128[...].T
    steps_parts = split3(steps_col)

    def onehot(quad):
        return jnp.where(
            iota((LANES, WIDE), 0) == iota((LANES, WIDE), 1) // width + quad * (WIDE // width), 1.0, 0.0
        ).astype(BF16)

    def onehot_t(quad):
        return jnp.where(
            iota((WIDE, LANES), 1) == iota((WIDE, LANES), 0) // width + quad * (WIDE // width), 1.0, 0.0
        ).astype(BF16)

    @pl.loop(0, quads)
    def _(q):
        at = pl.ds(pl.multiple_of(q * WIDE, WIDE), WIDE)
        pick = onehot(q)
        run = nn(run_col[0], pick) + nn(run_col[1], pick) + nn(run_col[2], pick)
        run_s[:, at] = run
        steps_s[:, at] = nn(steps_parts[0], pick) + nn(steps_parts[1], pick) + nn(steps_parts[2], pick)
        fade = jnp.exp2(run[tok - 1 : tok])
        f_s[2 * q] = jnp.broadcast_to(fade[:, :LANES], (8, LANES))
        f_s[2 * q + 1] = jnp.broadcast_to(fade[:, LANES:], (8, LANES))

    @pl.when(has_prev)
    def _():
        halo_copy.wait_recv()
        ext[0:8] = halo_in[8:16].astype(F32)

    @pl.when(jnp.logical_not(has_prev))
    def _():
        ext[0:8] = jnp.zeros((8, chan), F32)

    def front(q):
        at = pl.ds(pl.multiple_of(q * WIDE, WIDE), WIDE)
        ext[8 : tok + 8, at] = xin[:, at].astype(F32)
        value = jnp.broadcast_to(conv_b[:, at], (tok, WIDE))
        for k in range(4):
            value = value + conv_w[k : k + 1, at] * ext[5 + k : 5 + k + tok, at]
        gate = 1.0 / (1.0 + jnp.exp(-value))
        x_s[:, at] = value * gate
        ds_s[:, at] = gate * (1.0 + value * (1.0 - gate))

    front(quads)
    writes = x_s[:, inner : inner + LANES]
    reads = x_s[:, inner + LANES :]
    b2 = split2(writes)
    c2 = split2(reads)
    ct2 = split2(reads.T)

    @pl.loop(0, quads)
    def _(q):
        at = pl.ds(pl.multiple_of(q * WIDE, WIDE), WIDE)
        w = split2(jnp.exp2(run_s[:, at]) * cot[:, at].astype(F32))
        g = both(nn, ct2, w)
        gt[2 * q] = g[:, :LANES]
        gt[2 * q + 1] = g[:, LANES:]

    def chunk(p):
        return pltpu.make_async_remote_copy(
            src_ref=gt.at[p], dst_ref=et.at[p],
            send_sem=send_sem.at[p], recv_sem=recv_sem.at[p],
            device_id=to(idx - 1), device_id_type=MESH,
        )

    def chain():
        @pl.loop(0, pairs)
        def _(p):
            @pl.when(has_next)
            def _():
                chunk(p).wait_recv()
                gt[p] = gt[p] + f_s[p][0:1] * et[p]

            @pl.when(jnp.logical_not(has_next))
            def _():
                et[p] = jnp.zeros((LANES, LANES), F32)

            @pl.when(has_prev)
            def _():
                chunk(p).start()

    early = idx >= n // 2

    @pl.when(early)
    def _():
        chain()

    gram[...] = both(nt, b2, c2)
    dgram[...] = jnp.zeros_like(dgram)
    acc_c[...] = jnp.zeros_like(acc_c)
    acc_b[...] = jnp.zeros_like(acc_b)
    q_acc[...] = jnp.zeros_like(q_acc)
    r_acc[...] = jnp.zeros_like(r_acc)
    last_acc[...] = jnp.zeros_like(last_acc)
    skip_acc[...] = jnp.zeros_like(skip_acc)
    dpos[...] = jnp.zeros_like(dpos)

    @pl.loop(0, quads)
    def _(q):
        at = pl.ds(pl.multiple_of(q * WIDE, WIDE), WIDE)
        front(q)
        dy = cot[:, at].astype(F32)
        w = jnp.exp2(run_s[:, at]) * dy
        st = state[at, :].T
        hi, lo = split2(st)
        st_hi[:, at] = hi
        st_lo[:, at] = lo
        acc_c[...] += both(nt, split2(w), (hi, lo))
        zy = split2(both(nn, c2, (hi, lo)) * w)
        pick = onehot_t(q)
        r_acc[...] += nn(zy[0], pick) + nn(zy[1], pick)
        sk = split2(jnp.broadcast_to(jnp.sum(dy * x_s[:, at], axis=0, keepdims=True), (8, WIDE)))
        skip_acc[...] += nn(sk[0], pick) + nn(sk[1], pick)

    low = iota((tok, LANES), 1) < width
    mask = iota((tok, tok), 0) <= iota((tok, tok), 1)

    @pl.loop(0, pairs)
    def _(p):
        at = pl.ds(pl.multiple_of(p * LANES, LANES), LANES)
        dy = cot[:, at]
        dy_f = dy.astype(F32)
        xs = x_s[:, at] * steps_s[:, at]
        run = run_s[:, at]
        turned = pltpu.roll(run, width, 1)
        twice = jnp.concatenate([dy, dy], axis=1)
        total = jnp.zeros((tok, LANES), F32)
        for half in range(2):
            mine = low if half == 0 else jnp.logical_not(low)
            x_hi, x_lo = split2(jnp.where(mine, xs, 0.0))
            dm = nt(jnp.concatenate([x_hi, x_lo], axis=1), twice)
            own = jnp.where(mine, run, turned)
            own = jnp.concatenate([own, own], axis=1)
            gap = run_t[pl.ds(2 * p + half, 1), :] - own
            fade = jnp.exp2(jnp.where(mask, gap, -jnp.inf))
            ldm = fade * dm
            dgram[...] += ldm
            m = fade * gram[...]
            dpos[pl.ds(2 * p + half, 1), :] = jnp.sum(m * dm, axis=0, keepdims=True)
            m_hi, m_lo = split2(m)
            dy_m = jnp.where(mine, dy_f, 0.0).astype(BF16)
            total = total + nn(m_hi, dy_m) + nn(m_lo, dy_m)
        dxs_s[:, at] = total

    @pl.when(jnp.logical_not(early))
    def _():
        chain()

    @pl.loop(0, quads)
    def _(q):
        at = pl.ds(pl.multiple_of(q * WIDE, WIDE), WIDE)
        e = jnp.concatenate([et[2 * q], et[2 * q + 1]], axis=1)
        e2 = split2(e)
        run = run_s[:, at]
        remain = jnp.exp2(run[tok - 1 : tok] - run)
        rv = remain * both(nn, b2, e2)
        steps = steps_s[:, at]
        x = x_s[:, at]
        dxs = rv + dxs_s[:, at]
        xs = x * steps
        pick = onehot_t(q)
        part = split2(x * dxs)
        q_acc[...] += nn(part[0], pick) + nn(part[1], pick)
        st = st_hi[:, at].astype(F32) + st_lo[:, at].astype(F32)
        fade = jnp.exp2(run[tok - 1 : tok])
        end = jnp.sum(xs * rv, axis=0, keepdims=True) + fade * jnp.sum(e * st, axis=0, keepdims=True)
        end = split3(jnp.broadcast_to(end, (8, WIDE)))
        last_acc[...] += nn(end[0], pick) + nn(end[1], pick) + nn(end[2], pick)
        acc_b[...] += both(nt, split2(xs * remain), e2)
        lane = iota((1, WIDE), 1) // width
        gain = jnp.zeros((1, WIDE), F32)
        for j in range(WIDE // width):
            gain = jnp.where(lane == j, skip[q * (WIDE // width) + j], gain)
        dx = dxs * steps + gain * cot[:, at].astype(F32)
        dconv[0:tok, at] = dx * ds_s[:, at]

    dg = split2(dgram[...])
    dgt = split2(dgram[...].T)
    tail = pl.ds(inner, LANES)
    dconv[0:tok, tail] = (acc_b[...] + both(nn, dg, c2)) * ds_s[:, tail]
    tail = pl.ds(inner + LANES, LANES)
    dconv[0:tok, tail] = (acc_c[...] + both(nn, dgt, b2)) * ds_s[:, tail]

    back = pltpu.make_async_remote_copy(
        src_ref=dconv.at[pl.ds(0, 8)], dst_ref=dconv.at[pl.ds(tok, 8)],
        send_sem=back_sem.at[0], recv_sem=back_sem.at[1],
        device_id=to(idx - 1), device_id_type=MESH,
    )

    @pl.when(has_prev)
    def _():
        back.start()

    @pl.when(jnp.logical_not(has_next))
    def _():
        dconv[tok : tok + 8] = jnp.zeros((8, chan), F32)

    drun = r_acc[...] - steps_col * q_acc[...]
    drun = drun + jnp.where(iota((tok, LANES), 0) == tok - 1, last_acc[0:1, :], 0.0)
    dp = split3(drun.T + dpos[...])
    ddecay = (nn(dp[0], lower) + nn(dp[1], lower) + nn(dp[2], lower))[0:heads]
    dsteps = q_acc[...].T[0:heads] - ddecay * rate
    sg = dsteps / (1.0 + jnp.exp(-z))
    step_g[...] = sg
    p128[0:heads, :] = sg
    bf_buf[0, 5:6, 0:LANES] = jnp.sum(p128[...].T, axis=0, keepdims=True)
    p128[0:heads, :] = -ddecay * steps_t * rate
    bf_buf[0, 5:6, LANES : 2 * LANES] = jnp.sum(p128[...].T, axis=0, keepdims=True)
    bf_buf[0, 5:6, 2 * LANES : 3 * LANES] = skip_acc[0:1]
    bf_buf[0, 5:6, 3 * LANES :] = jnp.zeros((1, chan - 3 * LANES), F32)
    bf_buf[0, 6:8, :] = jnp.zeros((2, chan), F32)

    @pl.loop(0, chan // LANES)
    def _(q):
        at = pl.ds(pl.multiple_of(q * LANES, LANES), LANES)
        d = dconv[0:tok, at]
        for k in range(4):
            bf_buf[0, k : k + 1, at] = jnp.sum(d * ext[5 + k : 5 + k + tok, at], axis=0, keepdims=True)
        bf_buf[0, 4:5, at] = jnp.sum(d, axis=0, keepdims=True)

    def swap(k):
        return pltpu.make_async_remote_copy(
            src_ref=bf_buf.at[k], dst_ref=bf_in.at[k],
            send_sem=sum_sem.at[k], recv_sem=sum_sem.at[rounds + k],
            device_id=to(partner(k)), device_id_type=MESH,
        )

    swap(0).start()

    @pl.when(has_next)
    def _():
        back.wait_recv()

    @pl.loop(0, chan // LANES)
    def _(q):
        at = pl.ds(pl.multiple_of(q * LANES, LANES), LANES)
        value = conv_w[3:4, at] * dconv[0:tok, at]
        for k in range(3):
            value = value + conv_w[k : k + 1, at] * dconv[3 - k : 3 - k + tok, at]
        ig[:, at] = value

    for k in range(rounds):
        swap(k).wait_recv()
        bf_buf[k + 1] = bf_buf[k] + bf_in[k]
        if k + 1 < rounds:
            swap(k + 1).start()
    kg_out[...] = bf_buf[rounds, 0:4]
    off_out[...] = bf_buf[rounds, 4:5]
    for j in range(3):
        small_out[j : j + 1, :] = bf_buf[rounds, 5:6, j * LANES : (j + 1) * LANES]

    for k in range(rounds):
        swap(k).wait_send()

    @pl.when(has_next)
    def _():
        halo_copy.wait_send()

    @pl.when(has_prev)
    def _():
        back.wait_send()

        @pl.loop(0, pairs)
        def _(p):
            chunk(p).wait_send()


def per_device(
    mixed_input, step_raw, conv_weight, conv_bias, step_bias, decay_log, skip_gain, result_cotangent, entry_state
):
    tok, chan = mixed_input.shape
    _, heads, width, span = entry_state.shape
    inner = heads * width
    n = lax.axis_size("seq")
    rounds = n.bit_length() - 1
    pairs = inner // LANES
    cols = jnp.stack([step_bias, decay_log], axis=1)
    vmem = pl.BlockSpec(memory_space=pltpu.VMEM)
    scr = lambda *shape: pltpu.VMEM(shape, F32)
    outs = pl.pallas_call(
        functools.partial(body, n, heads, width),
        out_shape=(
            jax.ShapeDtypeStruct((tok, chan), F32),
            jax.ShapeDtypeStruct((heads, tok), F32),
            jax.ShapeDtypeStruct((4, chan), F32),
            jax.ShapeDtypeStruct((1, chan), F32),
            jax.ShapeDtypeStruct((3, LANES), F32),
        ),
        in_specs=[vmem] * 5 + [pl.BlockSpec(memory_space=pltpu.SMEM)] + [vmem] * 2,
        out_specs=(vmem,) * 5,
        scratch_shapes=[
            scr(tok + 8, chan),
            scr(tok, chan),
            scr(tok, chan),
            scr(tok, inner),
            scr(tok, inner),
            scr(LANES, tok),
            scr(LANES, tok),
            scr(tok, inner),
            pltpu.VMEM((span, inner), BF16),
            pltpu.VMEM((span, inner), BF16),
            scr(pairs, span, LANES),
            scr(pairs, span, LANES),
            scr(pairs, 8, LANES),
            scr(tok, tok),
            scr(tok, tok),
            scr(LANES, tok),
            scr(tok, LANES),
            scr(tok, LANES),
            scr(tok, LANES),
            scr(tok, LANES),
            scr(8, LANES),
            scr(8, LANES),
            scr(tok + 8, chan),
            pltpu.VMEM((16, chan), BF16),
            scr(rounds + 1, 8, chan),
            scr(rounds, 8, chan),
            pltpu.SemaphoreType.DMA((pairs,)),
            pltpu.SemaphoreType.DMA((pairs,)),
            pltpu.SemaphoreType.DMA((2,)),
            pltpu.SemaphoreType.DMA((2,)),
            pltpu.SemaphoreType.DMA((2 * rounds,)),
        ],
        compiler_params=pltpu.CompilerParams(
            collective_id=0, has_side_effects=True, vmem_limit_bytes=60 * 1024 * 1024
        ),
    )(
        mixed_input, step_raw, conv_weight, conv_bias.reshape(1, chan), cols, skip_gain,
        result_cotangent, entry_state.reshape(inner, span),
    )
    grad, step_g, kg, off, small = outs
    return (grad, step_g, kg, off[0], small[0, :heads], small[1, :heads], small[2, :heads])


def solution(mesh):
    rows = ("groups", "seq")
    return jax.shard_map(
        per_device,
        mesh=mesh,
        in_specs=(
            P(rows, None), P(None, rows), P(), P(), P(), P(), P(), P(rows, None), P(rows, None, None, None),
        ),
        out_specs=(P(rows, None), P(None, rows), P("groups", None), P("groups"), P("groups"), P("groups"), P("groups")),
        check_vma=False,
    )
```

profile of v0, /device:TPU:14, one launch (start us, length us, event | category | flops | bytes accessed | tf_op | source)
XLA Modules:
  0.0 91.5 jit_solution(994362111074198502)
XLA Ops:
  0.6 0.7 pad_maximum_fusion
  1.3 0.7 copy.18.cols
  2.0 1.3 %reshape.20.conv_b = f32[1,2816]{1,0:T(1,128)} reshape(f32[2816]{0:T(1024)} %param.12) | data formatting | bytes 22528 | tf_op jit(solution)/shard_map/reshape | solution.py:433
  3.3 80.7 %shard_map.144 = (f32[256,2816]{1,0:T(8,128)}, f32[40,256]{1,0:T(8,128)}, f32[4,2816]{1,0:T(4,128)}, f32[1,2816]{1,0:T(1,128)}, f32[3,128]{1,0:T(4,128)}) custom-call(bf16[256,2816]{1,0:T(8,128)(2,1)} %xin.1, f32[40,256]{1,0:T(8,128)} %raw.1, f32[4,2816]{1,0:T(4,128)} %conv_w.1, f32[1,2816]{1,0:T(1,128)} %reshape.20.conv_b, f32[40,2]{1,0:T(8,128)} %copy.18.cols, ...), custom_call_target="tpu_custom_call" | custom-call | tf_op jit(solution)/shard_map/pallas_call | solution.py:385
  84.0 1.3 %slice_bitcast_fusion = (f32[40]{0:T(128)}, f32[40]{0:T(128)}, f32[40]{0:T(128)}) fusion(f32[3,128]{1,0:T(4,128)} %get-tuple-element.16), kind=kLoop, calls=%fused_computation.1 | loop fusion | bytes 960 | tf_op jit(solution)/shard_map/squeeze | solution.py:437
  85.3 1.3 %reduce = f32[2816]{0:T(1024)} reduce(f32[1,2816]{1,0:T(1,128)} %get-tuple-element.15, f32[]{:T(128)} %constant.1), dimensions={0}, to_apply=%get-tuple-element.15.reduce_sub_computation | reduce | bytes 22532 | tf_op jit(solution)/shard_map/pallas_call | solution.py:385
  86.6 0.0 copy-start.1
  86.6 0.0 copy-start
  86.7 3.6 %copy.22 = f32[256,2816]{1,0:T(8,128)} copy(f32[256,2816]{1,0:T(8,128)} %get-tuple-element.27) | data formatting | bytes 5767168
  90.2 0.0 copy-done.1
  90.2 0.6 copy.23
  90.9 0.0 copy-done
  90.9 0.6 copy.24
Async XLA Ops:
  86.6 3.6 %copy-start.1 = (f32[40,256]{1,0:T(8,128)S(1)}, f32[40,256]{1,0:T(8,128)}, u32[]{:S(2)}) copy-start(f32[40,256]{1,0:T(8,128)} %get-tuple-element.28) | copy-start | bytes 122884
  86.6 4.2 %copy-start = (f32[4,2816]{1,0:T(4,128)S(1)}, f32[4,2816]{1,0:T(4,128)}, u32[]{:S(2)}) copy-start(f32[4,2816]{1,0:T(4,128)} %get-tuple-element.29) | copy-start | bytes 135172
where the time goes:
time: 91.8 us; the launch traced here: 91.5 us
  Pallas kernels  80.7 us (88%)
  local copies, waits for them, and re-layouts  8.1 us (9%)
  other arithmetic  2.01 us (2%)
    pallas_call x1, Pallas kernels, per_device(): pl.pallas_call(functools.partial(body, n, heads, width), out_shape=(jax.S...  80.7 us
    unnamed x7, local copies, waits for them, and re-layouts  4.83 us

commit v1 on v0

--- a/solution.py
+++ b/solution.py
@@ -45,10 +45,10 @@
 
 def body(
     n, heads, width,
-    xin, raw, conv_w, conv_b, cols, skip, cot, state,
-    ig, step_g, kg_out, off_out, small_out,
+    xin, raw, conv_w, conv_b1, bias, decay, skip, cot, state,
+    ig, step_g, sums_out,
     ext, x_s, ds_s, run_s, steps_s, p128, run_t, dxs_s, st_hi, st_lo, gt, et, f_s,
-    gram, dgram, dpos, acc_c, acc_b, q_acc, r_acc, last_acc, skip_acc, dconv, halo_in, bf_buf, bf_in,
+    gram, dgram, dpos, acc_c, acc_b, q_acc, r_acc, last_acc, skip_acc, dconv, conv_b, z_s, rate_s, halo_in, bf_buf, bf_in,
     send_sem, recv_sem, halo_sem, back_sem, sum_sem,
 ):
     tok = xin.shape[0]
@@ -91,9 +91,17 @@
     def _():
         halo_copy.start()
 
-    z = raw[...] + cols[:, 0:1]
+    conv_b[...] = conv_b1[...].reshape(1, chan)
+
+    @pl.loop(0, heads)
+    def _(h):
+        at = pl.ds(h, 1)
+        z_s[at] = raw[at] + bias[h]
+        rate_s[at] = jnp.exp(jnp.full((1, tok), decay[h], F32))
+
+    z = z_s[...]
     steps_t = jnp.maximum(z, 0.0) + jnp.log1p(jnp.exp(-jnp.abs(z)))
-    rate = jnp.exp(cols[:, 1:2])
+    rate = rate_s[...]
     p128[...] = jnp.zeros_like(p128)
     p128[0:heads, :] = -steps_t * rate * LOG2E
     upper = jnp.where(iota((tok, tok), 0) <= iota((tok, tok), 1), 1.0, 0.0).astype(BF16)
@@ -122,7 +130,6 @@
         pick = onehot(q)
         run = nn(run_col[0], pick) + nn(run_col[1], pick) + nn(run_col[2], pick)
         run_s[:, at] = run
-        steps_s[:, at] = nn(steps_parts[0], pick) + nn(steps_parts[1], pick) + nn(steps_parts[2], pick)
         fade = jnp.exp2(run[tok - 1 : tok])
         f_s[2 * q] = jnp.broadcast_to(fade[:, :LANES], (8, LANES))
         f_s[2 * q + 1] = jnp.broadcast_to(fade[:, LANES:], (8, LANES))
@@ -168,27 +175,21 @@
             device_id=to(idx - 1), device_id_type=MESH,
         )
 
-    def chain():
-        @pl.loop(0, pairs)
-        def _(p):
-            @pl.when(has_next)
-            def _():
-                chunk(p).wait_recv()
-                gt[p] = gt[p] + f_s[p][0:1] * et[p]
-
-            @pl.when(jnp.logical_not(has_next))
-            def _():
-                et[p] = jnp.zeros((LANES, LANES), F32)
-
-            @pl.when(has_prev)
-            def _():
-                chunk(p).start()
-
-    early = idx >= n // 2
-
-    @pl.when(early)
-    def _():
-        chain()
+    def serve(p):
+        @pl.when(has_next)
+        def _():
+            chunk(p).wait_recv()
+            gt[p] = gt[p] + f_s[p][0:1] * et[p]
+
+        @pl.when(jnp.logical_not(has_next))
+        def _():
+            et[p] = jnp.zeros((LANES, LANES), F32)
+
+        @pl.when(has_prev)
+        def _():
+            chunk(p).start()
+
+    slot = jnp.minimum((n - 1 - idx) * 4 // 5, quads)
 
     gram[...] = both(nt, b2, c2)
     dgram[...] = jnp.zeros_like(dgram)
@@ -200,28 +201,10 @@
     skip_acc[...] = jnp.zeros_like(skip_acc)
     dpos[...] = jnp.zeros_like(dpos)
 
-    @pl.loop(0, quads)
-    def _(q):
-        at = pl.ds(pl.multiple_of(q * WIDE, WIDE), WIDE)
-        front(q)
-        dy = cot[:, at].astype(F32)
-        w = jnp.exp2(run_s[:, at]) * dy
-        st = state[at, :].T
-        hi, lo = split2(st)
-        st_hi[:, at] = hi
-        st_lo[:, at] = lo
-        acc_c[...] += both(nt, split2(w), (hi, lo))
-        zy = split2(both(nn, c2, (hi, lo)) * w)
-        pick = onehot_t(q)
-        r_acc[...] += nn(zy[0], pick) + nn(zy[1], pick)
-        sk = split2(jnp.broadcast_to(jnp.sum(dy * x_s[:, at], axis=0, keepdims=True), (8, WIDE)))
-        skip_acc[...] += nn(sk[0], pick) + nn(sk[1], pick)
-
     low = iota((tok, LANES), 1) < width
     mask = iota((tok, tok), 0) <= iota((tok, tok), 1)
 
-    @pl.loop(0, pairs)
-    def _(p):
+    def pair(p):
         at = pl.ds(pl.multiple_of(p * LANES, LANES), LANES)
         dy = cot[:, at]
         dy_f = dy.astype(F32)
@@ -247,13 +230,45 @@
             total = total + nn(m_hi, dy_m) + nn(m_lo, dy_m)
         dxs_s[:, at] = total
 
-    @pl.when(jnp.logical_not(early))
-    def _():
-        chain()
-
     @pl.loop(0, quads)
     def _(q):
         at = pl.ds(pl.multiple_of(q * WIDE, WIDE), WIDE)
+
+        @pl.when(q == slot)
+        def _():
+            @pl.loop(0, pairs)
+            def _(p):
+                serve(p)
+
+        front(q)
+        pick = onehot(q)
+        steps_s[:, at] = nn(steps_parts[0], pick) + nn(steps_parts[1], pick) + nn(steps_parts[2], pick)
+        dy = cot[:, at].astype(F32)
+        w = jnp.exp2(run_s[:, at]) * dy
+        st = state[at, :].T
+        hi, lo = split2(st)
+        st_hi[:, at] = hi
+        st_lo[:, at] = lo
+        acc_c[...] += both(nt, split2(w), (hi, lo))
+        zy = split2(both(nn, c2, (hi, lo)) * w)
+        pick = onehot_t(q)
+        r_acc[...] += nn(zy[0], pick) + nn(zy[1], pick)
+        sk = split2(jnp.broadcast_to(jnp.sum(dy * x_s[:, at], axis=0, keepdims=True), (8, WIDE)))
+        skip_acc[...] += nn(sk[0], pick) + nn(sk[1], pick)
+
+        @pl.loop(0, 2)
+        def _(j):
+            pair(2 * q + j)
+
+    @pl.loop(0, quads)
+    def _(q):
+        at = pl.ds(pl.multiple_of(q * WIDE, WIDE), WIDE)
+
+        @pl.when(slot == quads)
+        def _():
+            serve(2 * q)
+            serve(2 * q + 1)
+
         e = jnp.concatenate([et[2 * q], et[2 * q + 1]], axis=1)
         e2 = split2(e)
         run = run_s[:, at]
@@ -349,10 +364,7 @@
         bf_buf[k + 1] = bf_buf[k] + bf_in[k]
         if k + 1 < rounds:
             swap(k + 1).start()
-    kg_out[...] = bf_buf[rounds, 0:4]
-    off_out[...] = bf_buf[rounds, 4:5]
-    for j in range(3):
-        small_out[j : j + 1, :] = bf_buf[rounds, 5:6, j * LANES : (j + 1) * LANES]
+    sums_out[...] = bf_buf[rounds]
 
     for k in range(rounds):
         swap(k).wait_send()
@@ -368,6 +380,33 @@
         @pl.loop(0, pairs)
         def _(p):
             chunk(p).wait_send()
+
+
+def finish(sums, sg, made, ig, kg, off, step_g, bias_g, decay_g, skip_g, held, load_sem, store_sem):
+    pieces = load_sem.shape[0]
+    rows = held.shape[0] // pieces
+
+    def load(k):
+        at = pl.ds(k * rows, rows)
+        return pltpu.make_async_copy(made.at[at], held.at[at], load_sem.at[k])
+
+    def store(k):
+        at = pl.ds(k * rows, rows)
+        return pltpu.make_async_copy(held.at[at], ig.at[at], store_sem.at[k])
+
+    for k in range(pieces):
+        load(k).start()
+    kg[...] = sums[0:4]
+    off[...] = sums[4:5].reshape(off.shape)
+    step_g[...] = sg[...]
+    for j, ref in enumerate((bias_g, decay_g, skip_g)):
+        row = sums[5:6, j * LANES : (j + 1) * LANES]
+        ref[...] = row.reshape(LANES)[: ref.shape[0]]
+    for k in range(pieces):
+        load(k).wait()
+        store(k).start()
+    for k in range(pieces):
+        store(k).wait()
 
 
 def per_device(
@@ -379,20 +418,18 @@
     n = lax.axis_size("seq")
     rounds = n.bit_length() - 1
     pairs = inner // LANES
-    cols = jnp.stack([step_bias, decay_log], axis=1)
     vmem = pl.BlockSpec(memory_space=pltpu.VMEM)
+    smem = pl.BlockSpec(memory_space=pltpu.SMEM)
     scr = lambda *shape: pltpu.VMEM(shape, F32)
     outs = pl.pallas_call(
         functools.partial(body, n, heads, width),
         out_shape=(
             jax.ShapeDtypeStruct((tok, chan), F32),
             jax.ShapeDtypeStruct((heads, tok), F32),
-            jax.ShapeDtypeStruct((4, chan), F32),
-            jax.ShapeDtypeStruct((1, chan), F32),
-            jax.ShapeDtypeStruct((3, LANES), F32),
+            jax.ShapeDtypeStruct((8, chan), F32),
         ),
-        in_specs=[vmem] * 5 + [pl.BlockSpec(memory_space=pltpu.SMEM)] + [vmem] * 2,
-        out_specs=(vmem,) * 5,
+        in_specs=[vmem] * 4 + [smem] * 3 + [vmem] * 2,
+        out_specs=(vmem,) * 3,
         scratch_shapes=[
             scr(tok + 8, chan),
             scr(tok, chan),
@@ -417,6 +454,9 @@
             scr(8, LANES),
             scr(8, LANES),
             scr(tok + 8, chan),
+            scr(1, chan),
+            scr(heads, tok),
+            scr(heads, tok),
             pltpu.VMEM((16, chan), BF16),
             scr(rounds + 1, 8, chan),
             scr(rounds, 8, chan),
@@ -430,11 +470,28 @@
             collective_id=0, has_side_effects=True, vmem_limit_bytes=60 * 1024 * 1024
         ),
     )(
-        mixed_input, step_raw, conv_weight, conv_bias.reshape(1, chan), cols, skip_gain,
+        mixed_input, step_raw, conv_weight, conv_bias, step_bias, decay_log, skip_gain,
         result_cotangent, entry_state.reshape(inner, span),
     )
-    grad, step_g, kg, off, small = outs
-    return (grad, step_g, kg, off[0], small[0, :heads], small[1, :heads], small[2, :heads])
+    made, sg, sums = outs
+    hbm = pl.BlockSpec(memory_space=pl.ANY)
+    ig, kg, off, step_g, bias_g, decay_g, skip_g = pl.pallas_call(
+        finish,
+        out_shape=(
+            jax.ShapeDtypeStruct((tok, chan), F32),
+            jax.ShapeDtypeStruct((4, chan), F32),
+            jax.ShapeDtypeStruct((chan,), F32),
+            jax.ShapeDtypeStruct((heads, tok), F32),
+            jax.ShapeDtypeStruct((heads,), F32),
+            jax.ShapeDtypeStruct((heads,), F32),
+            jax.ShapeDtypeStruct((heads,), F32),
+        ),
+        in_specs=[vmem, vmem, hbm],
+        out_specs=(hbm,) + (vmem,) * 6,
+        scratch_shapes=[scr(tok, chan), pltpu.SemaphoreType.DMA((8,)), pltpu.SemaphoreType.DMA((8,))],
+        compiler_params=pltpu.CompilerParams(vmem_limit_bytes=60 * 1024 * 1024),
+    )(sums, sg, made)
+    return ig, step_g, kg, off, bias_g, decay_g, skip_g
 
 
 def solution(mesh):

time: 91.8 us -> 80.4 us (0.88)
  the two profiles are of different devices: /device:TPU:14 before, /device:TPU:24 now
where the time goes in v1:
time: 80.4 us; the launch traced here: 80.2 us
  Pallas kernels  79.6 us (99%)
    pallas_call x1, Pallas kernels, per_device(): pl.pallas_call(functools.partial(body, n, heads, width), out_shape=(jax.S...  75.3 us
    pallas_call x1, Pallas kernels, per_device(): pl.pallas_call(finish, out_shape=(jax.ShapeDtypeStruct((tok, chan), F32),...  4.23 us

profile of v1, /device:TPU:24, one launch (start us, length us, event | category | flops | bytes accessed | tf_op | source)
XLA Modules:
  0.0 80.2 jit_solution(3959312081664999162)
XLA Ops:
  0.6 75.3 %shard_map.144 = (f32[256,2816]{1,0:T(8,128)}, f32[40,256]{1,0:T(8,128)}, f32[8,2816]{1,0:T(8,128)}) custom-call(bf16[256,2816]{1,0:T(8,128)(2,1)} %xin.1, f32[40,256]{1,0:T(8,128)} %raw.1, f32[4,2816]{1,0:T(4,128)} %conv_w.1, f32[2816]{0:T(1024)} %conv_b1.1, f32[40]{0:T(128)} %bias.1, f32[40]{0:T(128)} %decay.1, f32[40]{0:T(128)} %skip.1, ...), custom_call_target="tpu_custom_call" | custom-call | tf_op jit(solution)/shard_map/pallas_call | solution.py:424
  76.0 4.2 %shard_map.145 = (f32[256,2816]{1,0:T(8,128)}, f32[4,2816]{1,0:T(4,128)}, f32[2816]{0:T(1024)}, f32[40,256]{1,0:T(8,128)}, f32[40]{0:T(128)}, /*index=5*/f32[40]{0:T(128)}, f32[40]{0:T(128)}) custom-call(f32[8,2816]{1,0:T(8,128)} %get-tuple-element.17.sums, f32[40,256]{1,0:T(8,128)} %get-tuple-element.18.sg, f32[256,2816]{1,0:T(8,128)} %get-tuple-element.19.made), custom_call_target="tpu_custom_call" | custom-call | tf_op jit(solution)/shard_map/pallas_call | solution.py:478
